TPU v7x, 256 devices: a whole 4x4x8 slice. The times are simulated.
256 devices in a mesh: dp: 16 (over z_hi, x), blk: 16 (over y, z_lo, core).
Axes of the slice: x: 4, y: 4, z: 8 (z_hi: 4, z_lo: 2; z = z_hi * 2 + z_lo), core: 2. Of those that a mesh axis runs over, the one named last changes fastest.
Arguments:
- queries: bfloat16 [16, 2048, 2048], P('dp', 'blk'), may hold values from -6 to 6
- keys: bfloat16 [16, 2048, 512], P('dp', 'blk'), may hold values from -6 to 6
- values: bfloat16 [16, 2048, 512], P('dp', 'blk'), may hold values from -6 to 6
- out_grad: bfloat16 [16, 2048, 2048], P('dp', 'blk'), may hold values from -6 to 6
- layer_input: bfloat16 [16, 2048, 4096], P('dp', 'blk'), may hold values from -6 to 6
- lengths: int32 [16, 3], P('dp'), may hold values from 128 to 1792, as said below
Outputs:
- query_grad: bfloat16 [16, 2048, 2048], P('dp', 'blk')
- key_grad: bfloat16 [16, 2048, 512], P('dp', 'blk')
- value_grad: bfloat16 [16, 2048, 512], P('dp', 'blk')
- weight_grad: float32 [4096, 1024], P(('dp', 'blk'))
Inputs may be any that keep to these rules, and one draw needn't show every extreme that they name: `lengths`: each row sums to 2048; the chosen and rejected counts lie between 128 and 384.
All inputs are finite; a program needn't handle non-finite values.
Results may differ from a plain program's by a relative error of at most 0.023.
Values may be sent and summed in bfloat16 or wider, within the bound.
A program may use at most 128 MiB of HBM per device.

v0:
```python
import math
import jax
import jax.numpy as jnp
from jax import lax
from jax.sharding import PartitionSpec as P

HEAD = 128
rope_base = 500000.0
masked_fill = -1e30


def side_by_side(arrays, axis, dim, along):
    widths = [a.shape[along] for a in arrays]
    both = jnp.concatenate(arrays, axis=along)
    whole = lax.all_gather(both, axis, axis=dim, tiled=True)
    return tuple(jnp.split(whole, [sum(widths[:k]) for k in range(1, len(widths))], axis=along))


def in_one_piece(arrays, axis, dim, along):
    widths = [a.shape[along] for a in arrays]
    both = jnp.concatenate(arrays, axis=along)
    whole = lax.psum_scatter(both, axis, scatter_dimension=dim, tiled=True)
    return tuple(jnp.split(whole, [sum(widths[:k]) for k in range(1, len(widths))], axis=along))


def cut_along(array, dim, count):
    before, after = (array.shape[:dim], array.shape[dim + 1 :])
    return jnp.moveaxis(array.reshape(*before, count, -1, *after), dim, 0)


def sum_at_owner(array, axis, dim):
    pieces = cut_along(array, dim, lax.axis_size(axis))
    arrived = lax.all_to_all(pieces, axis, split_axis=0, concat_axis=0, tiled=True)
    return arrived.astype(jnp.float32).sum(axis=0)


def stored_positions(stored_rows, shard_rows, shard_count):
    half_rows = shard_rows // 2
    block_number = stored_rows // half_rows
    holder = block_number // 2
    upper_half = block_number % 2
    position_block = jnp.where(upper_half == 1, 2 * shard_count - 1 - holder, holder)
    return (position_block * half_rows + stored_rows % half_rows).astype(jnp.int32)


def allowed_pairs(query_pos, key_pos, prompt_len, chosen_len):
    causal = key_pos[None, :] <= query_pos[:, None]
    reject_start = prompt_len + chosen_len
    query_rejected = query_pos >= reject_start
    key_chosen = jnp.logical_and(key_pos >= prompt_len, key_pos < reject_start)
    return jnp.logical_and(
        causal, jnp.logical_not(jnp.logical_and(query_rejected[:, None], key_chosen[None, :]))
    )


def block_length(total_rows):
    chosen_size = 1
    for candidate in range(1, min(total_rows, 512) + 1):
        if total_rows % candidate == 0:
            chosen_size = candidate
    return chosen_size


def over_blocks(running, pieces, first_row, block_fn):
    total_rows = pieces[0].shape[0]
    block_rows = block_length(total_rows)

    def one_turn(turn_index, current):
        block_start = turn_index * block_rows
        block_parts = tuple(
            (lax.dynamic_slice_in_dim(member, block_start, block_rows, 0) for member in pieces)
        )
        return block_fn(current, block_parts, first_row + block_start)

    return lax.fori_loop(0, total_rows // block_rows, one_turn, running)


def keep_state(running):
    return running


def body(queries, keys, values, out_grad, layer_input, lengths):
    shard_count = lax.axis_size("blk")
    shard_index = lax.axis_index("blk")
    shard_rows = queries.shape[1]
    kv_heads = keys.shape[2] // HEAD
    group_heads = queries.shape[2] // keys.shape[2]
    seq_len = shard_rows * shard_count
    query_count = group_heads * shard_rows
    scale = 1.0 / math.sqrt(HEAD)
    prompt_len = lengths[0, 0]
    chosen_len = lengths[0, 1]
    own_rows = shard_index * shard_rows + jnp.arange(shard_rows, dtype=jnp.int32)
    own_pos = stored_positions(own_rows, shard_rows, shard_count)
    query_pos = jnp.tile(own_pos, group_heads)
    query_rows = (
        queries[0]
        .reshape(shard_rows, kv_heads, group_heads, HEAD)
        .transpose(1, 2, 0, 3)
        .reshape(kv_heads, query_count, HEAD)
    )
    grad_rows = (
        out_grad[0]
        .reshape(shard_rows, kv_heads, group_heads, HEAD)
        .transpose(1, 2, 0, 3)
        .reshape(kv_heads, query_count, HEAD)
    )

    def block_allowed(first_row, count_rows):
        key_pos = stored_positions(
            first_row + jnp.arange(count_rows, dtype=jnp.int32), shard_rows, shard_count
        )
        return allowed_pairs(query_pos, key_pos, prompt_len, chosen_len)

    def forward_block(running, block_parts, first_row):
        key_block, value_block = block_parts
        count_rows = key_block.shape[0]
        allowed = block_allowed(first_row, count_rows)

        def forward_compute(current):
            run_max, run_sum, run_acc = current
            key_heads = key_block.reshape(count_rows, kv_heads, HEAD)
            value_heads = value_block.reshape(count_rows, kv_heads, HEAD).astype(jnp.float32)
            scores = scale * jnp.einsum(
                "gqe,kge->gqk", query_rows, key_heads, preferred_element_type=jnp.float32
            )
            new_max = jnp.maximum(
                run_max, jnp.max(jnp.where(allowed[None], scores, masked_fill), axis=-1)
            )
            weights = jnp.where(allowed[None], jnp.exp(scores - new_max[..., None]), 0.0)
            factor = jnp.exp(run_max - new_max)
            new_sum = run_sum * factor + jnp.sum(weights, axis=-1)
            new_acc = run_acc * factor[..., None] + jnp.einsum(
                "gqk,kge->gqe", weights, value_heads, precision=lax.Precision.HIGHEST
            )
            return (new_max, new_sum, new_acc)

        return lax.cond(jnp.any(allowed), forward_compute, keep_state, running)

    start_forward = (
        jnp.full((kv_heads, query_count), masked_fill, jnp.float32),
        jnp.zeros((kv_heads, query_count), jnp.float32),
        jnp.zeros((kv_heads, query_count, HEAD), jnp.float32),
    )
    run_max, run_sum, run_acc = over_blocks(
        start_forward, side_by_side((keys[0], values[0]), "blk", 0, 1), jnp.int32(0), forward_block
    )
    attn_out = run_acc / run_sum[..., None]
    log_total = run_max + jnp.log(run_sum)
    delta = jnp.sum(grad_rows.astype(jnp.float32) * attn_out, axis=-1)

    def backward_block(running, block_parts, first_row):
        key_block, value_block = block_parts
        count_rows = key_block.shape[0]
        allowed = block_allowed(first_row, count_rows)

        def backward_compute(current):
            query_acc, key_acc, value_acc = current
            key_heads = key_block.reshape(count_rows, kv_heads, HEAD)
            value_heads = value_block.reshape(count_rows, kv_heads, HEAD)
            scores = scale * jnp.einsum(
                "gqe,kge->gqk", query_rows, key_heads, preferred_element_type=jnp.float32
            )
            probs = jnp.where(allowed[None], jnp.exp(scores - log_total[..., None]), 0.0)
            prob_half = probs.astype(jnp.bfloat16)
            prob_grad = jnp.einsum(
                "gqe,kge->gqk", grad_rows, value_heads, preferred_element_type=jnp.float32
            )
            score_grad = (scale * probs * (prob_grad - delta[..., None])).astype(jnp.bfloat16)
            query_acc = query_acc + jnp.einsum(
                "gqk,kge->gqe", score_grad, key_heads, preferred_element_type=jnp.float32
            )
            key_term = jnp.einsum(
                "gqk,gqe->kge", score_grad, query_rows, preferred_element_type=jnp.float32
            ).reshape(count_rows, kv_heads * HEAD)
            value_term = jnp.einsum(
                "gqk,gqe->kge", prob_half, grad_rows, preferred_element_type=jnp.float32
            ).reshape(count_rows, kv_heads * HEAD)
            key_acc = lax.dynamic_update_slice_in_dim(
                key_acc,
                lax.dynamic_slice_in_dim(key_acc, first_row, count_rows, 0) + key_term,
                first_row,
                0,
            )
            value_acc = lax.dynamic_update_slice_in_dim(
                value_acc,
                lax.dynamic_slice_in_dim(value_acc, first_row, count_rows, 0) + value_term,
                first_row,
                0,
            )
            return (query_acc, key_acc, value_acc)

        return lax.cond(jnp.any(allowed), backward_compute, keep_state, running)

    start_backward = (
        jnp.zeros((kv_heads, query_count, HEAD), jnp.float32),
        jnp.zeros((seq_len, kv_heads * HEAD), jnp.float32),
        jnp.zeros((seq_len, kv_heads * HEAD), jnp.float32),
    )
    query_acc, key_acc, value_acc = over_blocks(
        start_backward,
        side_by_side((keys[0], values[0]), "blk", 0, 1),
        jnp.int32(0),
        backward_block,
    )
    key_sum, value_sum = tuple(
        (
            part.astype(jnp.float32)
            for part in in_one_piece(
                (key_acc.astype(jnp.bfloat16), value_acc.astype(jnp.bfloat16)), "blk", 0, 1
            )
        )
    )
    query_grad = (
        query_acc.reshape(kv_heads, group_heads, shard_rows, HEAD)
        .transpose(2, 0, 1, 3)
        .reshape(shard_rows, kv_heads * group_heads * HEAD)
        .astype(jnp.bfloat16)
    )
    key_out = key_sum.astype(jnp.bfloat16)
    value_out = value_sum.astype(jnp.bfloat16)
    half_dim = HEAD // 2
    frequency = jnp.exp(
        -(2.0 * jnp.arange(half_dim, dtype=jnp.float32) / HEAD) * math.log(rope_base)
    )
    angles = own_pos.astype(jnp.float32)[:, None] * frequency[None, :]
    cosine = jnp.concatenate([jnp.cos(angles), jnp.cos(angles)], axis=-1)[:, None, :]
    sine = jnp.concatenate([jnp.sin(angles), jnp.sin(angles)], axis=-1)[:, None, :]
    grad_heads = key_sum.reshape(shard_rows, kv_heads, HEAD)
    rotated = jnp.concatenate([-grad_heads[..., half_dim:], grad_heads[..., :half_dim]], axis=-1)
    key_pre = (
        (grad_heads * cosine - rotated * sine)
        .reshape(shard_rows, kv_heads * HEAD)
        .astype(jnp.bfloat16)
    )
    grad_cols = jnp.concatenate([key_pre, value_out], axis=1)
    input_rows = layer_input[0]
    features = layer_input.shape[2]
    replica_count = lax.axis_size("dp")
    feature_share = features // (replica_count * shard_count)
    grouped_input = input_rows.reshape(shard_rows, replica_count, shard_count * feature_share)
    sequence_input = lax.all_to_all(grouped_input, "blk", split_axis=2, concat_axis=0, tiled=True)
    sequence_weight = jnp.einsum(
        "tif,tc->ifc",
        sequence_input,
        lax.all_gather(grad_cols, "blk", axis=0, tiled=True),
        preferred_element_type=jnp.float32,
    )
    weight_grad = sum_at_owner(sequence_weight.astype(jnp.bfloat16), "dp", 0).reshape(
        feature_share, grad_cols.shape[1]
    )
    return (query_grad[None], key_out[None], value_out[None], weight_grad)


def solution(mesh):
    placed = (
        P("dp", "blk", None),
        P("dp", "blk", None),
        P("dp", "blk", None),
        P("dp", "blk", None),
        P("dp", "blk", None),
        P("dp", None),
    )
    return jax.shard_map(
        body,
        mesh=mesh,
        in_specs=placed,
        out_specs=(
            P("dp", "blk", None),
            P("dp", "blk", None),
            P("dp", "blk", None),
            P(("dp", "blk"), None),
        ),
        check_vma=False,
    )
```

profile of v0, /device:TPU:1, one launch (start us, length us, event | category | flops | bytes accessed | tf_op | source)
XLA Modules:
  0.0 340.4 jit_solution(7980959696925305144)
XLA Ops:
  10.1 1.4 reshape_squeeze.9
  16.5 46.8 %all-gather.3.cloned.1.call-done = bf16[2048,1024]{0,1:T(8,128)(2,1)} async-done(((bf16[128,1024]{0,1:T(8,128)(2,1)}), bf16[2048,1024]{0,1:T(8,128)(2,1)}) %all-gather.3.cloned.1.call-update) | async-done | bytes 4194320 | tf_op jit(solution)/shard_map/all_gather | solution.py:15
  63.3 4.8 %fusion.55 = (bf16[2048,512]{0,1:T(8,128)(2,1)}, bf16[2048,512]{0,1:T(8,128)(2,1)}) fusion(bf16[2048,1024]{0,1:T(8,128)(2,1)} %all-gather.3.cloned.1.call-done), kind=kLoop, calls=%fused_computation.129 | loop fusion | bytes 8388608 | tf_op jit(solution)/shard_map/split | solution.py:16
  68.1 39.9 %while.44 = (s32[]{:T(128)}, f32[4,512]{1,0:T(4,128)S(1)}, f32[4,512]{1,0:T(4,128)S(1)}, f32[4,512,128]{2,1,0:T(8,128)S(1)}, s32[]{:T(128)}, /*index=5*/s32[]{:T...) while((s32[]{:T(128)}, f32[4,512]{1,0:T(4,128)S(1)}, ...), condition=%wide.region_6.7_spmd.clone.clone, body=%wide.region_0.6_spmd.clone.clone.sunk | while | flops 1891420160 | bytes 19541308 | solution.py:75
  70.4 7.7 %conditional.8 = ((f32[4,512]{1,0:T(4,128)S(1)}, f32[4,512]{1,0:T(4,128)S(1)}, f32[4,512,128]{2,1,0:T(8,128)S(1)})) conditional(s32[]{:T(128)} %convert_element_type.118, (f32[4,512]{1,0:T(4,128)S(1)}, f32[4,512]{1,0:T(4,128)S(1)}, f32[4,512,128]{2,1,0:T(8,128)S(1)}) %tuple.160, (pred[512,512]{0,1:T(8,128)(4,1)S(1)}, s32[]{:T(128)}, ...), branch_computations={%region_2.2_spmd, %region_3.5_spmd} | conditional | flops 1890062336 | bytes 19267654 | solution.py:138
  70.4 1.3 constant_dynamic-slice_fusion
  73.6 4.4 %fusion.18 = f32[4,512,128]{2,1,0:T(8,128)S(1)} fusion(bf16[512,4,128]{0,2,1:T(8,128)(2,1)S(1)} %bitcast.111, f32[4,512,512]{2,1,0:T(8,128)S(1)} %get-tuple-element.1214, f32[4,512]{1,0:T(4,128)S(1)} %max.5, pred[512,512]{0,1:T(8,128)(4,1)S(1)} %get-tuple-element.924, f32[4,512,128]{2,1,0:T(8,128)S(1)} %get-tuple-element.929, ...), kind=kOutput, calls=%fused_computation.15 | convolution fusion | flops 1614282752 | bytes 7094272 | tf_op jit(solution)/shard_map/while/body/eval_jaxpr/cond/branch_1_fun/gqk,kge->gqe/dot_general | solution.py:133
  80.3 7.7 %conditional.8 = ((f32[4,512]{1,0:T(4,128)S(1)}, f32[4,512]{1,0:T(4,128)S(1)}, f32[4,512,128]{2,1,0:T(8,128)S(1)})) conditional(s32[]{:T(128)} %convert_element_type.118, (f32[4,512]{1,0:T(4,128)S(1)}, f32[4,512]{1,0:T(4,128)S(1)}, f32[4,512,128]{2,1,0:T(8,128)S(1)}) %tuple.160, (pred[512,512]{0,1:T(8,128)(4,1)S(1)}, s32[]{:T(128)}, ...), branch_computations={%region_2.2_spmd, %region_3.5_spmd} | conditional | flops 1890062336 | bytes 19267654 | solution.py:138
  80.4 1.3 constant_dynamic-slice_fusion
  83.6 4.4 %fusion.18 = f32[4,512,128]{2,1,0:T(8,128)S(1)} fusion(bf16[512,4,128]{0,2,1:T(8,128)(2,1)S(1)} %bitcast.111, f32[4,512,512]{2,1,0:T(8,128)S(1)} %get-tuple-element.1214, f32[4,512]{1,0:T(4,128)S(1)} %max.5, pred[512,512]{0,1:T(8,128)(4,1)S(1)} %get-tuple-element.924, f32[4,512,128]{2,1,0:T(8,128)S(1)} %get-tuple-element.929, ...), kind=kOutput, calls=%fused_computation.15 | convolution fusion | flops 1614282752 | bytes 7094272 | tf_op jit(solution)/shard_map/while/body/eval_jaxpr/cond/branch_1_fun/gqk,kge->gqe/dot_general | solution.py:133
  90.3 7.7 %conditional.8 = ((f32[4,512]{1,0:T(4,128)S(1)}, f32[4,512]{1,0:T(4,128)S(1)}, f32[4,512,128]{2,1,0:T(8,128)S(1)})) conditional(s32[]{:T(128)} %convert_element_type.118, (f32[4,512]{1,0:T(4,128)S(1)}, f32[4,512]{1,0:T(4,128)S(1)}, f32[4,512,128]{2,1,0:T(8,128)S(1)}) %tuple.160, (pred[512,512]{0,1:T(8,128)(4,1)S(1)}, s32[]{:T(128)}, ...), branch_computations={%region_2.2_spmd, %region_3.5_spmd} | conditional | flops 1890062336 | bytes 19267654 | solution.py:138
  90.3 1.3 constant_dynamic-slice_fusion
  93.6 4.4 %fusion.18 = f32[4,512,128]{2,1,0:T(8,128)S(1)} fusion(bf16[512,4,128]{0,2,1:T(8,128)(2,1)S(1)} %bitcast.111, f32[4,512,512]{2,1,0:T(8,128)S(1)} %get-tuple-element.1214, f32[4,512]{1,0:T(4,128)S(1)} %max.5, pred[512,512]{0,1:T(8,128)(4,1)S(1)} %get-tuple-element.924, f32[4,512,128]{2,1,0:T(8,128)S(1)} %get-tuple-element.929, ...), kind=kOutput, calls=%fused_computation.15 | convolution fusion | flops 1614282752 | bytes 7094272 | tf_op jit(solution)/shard_map/while/body/eval_jaxpr/cond/branch_1_fun/gqk,kge->gqe/dot_general | solution.py:133
  100.3 7.7 %conditional.8 = ((f32[4,512]{1,0:T(4,128)S(1)}, f32[4,512]{1,0:T(4,128)S(1)}, f32[4,512,128]{2,1,0:T(8,128)S(1)})) conditional(s32[]{:T(128)} %convert_element_type.118, (f32[4,512]{1,0:T(4,128)S(1)}, f32[4,512]{1,0:T(4,128)S(1)}, f32[4,512,128]{2,1,0:T(8,128)S(1)}) %tuple.160, (pred[512,512]{0,1:T(8,128)(4,1)S(1)}, s32[]{:T(128)}, ...), branch_computations={%region_2.2_spmd, %region_3.5_spmd} | conditional | flops 1890062336 | bytes 19267654 | solution.py:138
  100.3 1.3 constant_dynamic-slice_fusion
  103.6 4.4 %fusion.18 = f32[4,512,128]{2,1,0:T(8,128)S(1)} fusion(bf16[512,4,128]{0,2,1:T(8,128)(2,1)S(1)} %bitcast.111, f32[4,512,512]{2,1,0:T(8,128)S(1)} %get-tuple-element.1214, f32[4,512]{1,0:T(4,128)S(1)} %max.5, pred[512,512]{0,1:T(8,128)(4,1)S(1)} %get-tuple-element.924, f32[4,512,128]{2,1,0:T(8,128)S(1)} %get-tuple-element.929, ...), kind=kOutput, calls=%fused_computation.15 | convolution fusion | flops 1614282752 | bytes 7094272 | tf_op jit(solution)/shard_map/while/body/eval_jaxpr/cond/branch_1_fun/gqk,kge->gqe/dot_general | solution.py:133
  108.4 1.2 multiply_reduce_fusion
  109.7 2.5 broadcast.1267
  112.2 2.5 broadcast.1267.clone
  114.7 53.3 %while.45 = (s32[]{:T(128)}, f32[4,512,128]{2,1,0:T(8,128)S(1)}, f32[2048,512]{0,1:T(8,128)}, f32[2048,512]{0,1:T(8,128)}, s32[]{:T(128)}, /*index=5*/s32[]{:T(1...) while((s32[]{:T(128)}, f32[4,512,128]{2,1,0:T(8,128)S(1)}, ...), condition=%wide.region_12.13_spmd.clone.clone, body=%wide.region_8.12_spmd.clone.clone.sunk | while | flops 1355855872 | bytes 35949944 | solution.py:75
  117.0 11.0 %conditional.9 = ((f32[4,512,128]{2,1,0:T(8,128)S(1)}, f32[2048,512]{0,1:T(8,128)}, f32[2048,512]{0,1:T(8,128)})) conditional(s32[]{:T(128)} %convert_element_type.119, (f32[4,512,128]{2,1,0:T(8,128)S(1)}, f32[2048,512]{0,1:T(8,128)}, f32[2048,512]{0,1:T(8,128)}) %tuple.165, (pred[512,512]{0,1:T(8,128)(4,1)S(1)}, s32[]{:T(128)}, ...), branch_computations={%region_10.10_spmd, %region_11.11_spmd} | conditional | flops 1354498048 | bytes 35676240 | solution.py:193
  120.0 1.7 fusion.23
  121.7 1.2 convolution_add_fusion
  124.7 3.3 constant_dynamic-update-slice_fusion
  130.4 11.0 %conditional.9 = ((f32[4,512,128]{2,1,0:T(8,128)S(1)}, f32[2048,512]{0,1:T(8,128)}, f32[2048,512]{0,1:T(8,128)})) conditional(s32[]{:T(128)} %convert_element_type.119, (f32[4,512,128]{2,1,0:T(8,128)S(1)}, f32[2048,512]{0,1:T(8,128)}, f32[2048,512]{0,1:T(8,128)}) %tuple.165, (pred[512,512]{0,1:T(8,128)(4,1)S(1)}, s32[]{:T(128)}, ...), branch_computations={%region_10.10_spmd, %region_11.11_spmd} | conditional | flops 1354498048 | bytes 35676240 | solution.py:193
  133.3 1.7 fusion.23
  135.0 1.2 convolution_add_fusion
  138.1 3.3 constant_dynamic-update-slice_fusion
  143.7 10.9 %conditional.9 = ((f32[4,512,128]{2,1,0:T(8,128)S(1)}, f32[2048,512]{0,1:T(8,128)}, f32[2048,512]{0,1:T(8,128)})) conditional(s32[]{:T(128)} %convert_element_type.119, (f32[4,512,128]{2,1,0:T(8,128)S(1)}, f32[2048,512]{0,1:T(8,128)}, f32[2048,512]{0,1:T(8,128)}) %tuple.165, (pred[512,512]{0,1:T(8,128)(4,1)S(1)}, s32[]{:T(128)}, ...), branch_computations={%region_10.10_spmd, %region_11.11_spmd} | conditional | flops 1354498048 | bytes 35676240 | solution.py:193
  146.7 1.7 fusion.23
  148.4 1.2 convolution_add_fusion
  151.4 3.2 constant_dynamic-update-slice_fusion
  157.0 10.9 %conditional.9 = ((f32[4,512,128]{2,1,0:T(8,128)S(1)}, f32[2048,512]{0,1:T(8,128)}, f32[2048,512]{0,1:T(8,128)})) conditional(s32[]{:T(128)} %convert_element_type.119, (f32[4,512,128]{2,1,0:T(8,128)S(1)}, f32[2048,512]{0,1:T(8,128)}, f32[2048,512]{0,1:T(8,128)}) %tuple.165, (pred[512,512]{0,1:T(8,128)(4,1)S(1)}, s32[]{:T(128)}, ...), branch_computations={%region_10.10_spmd, %region_11.11_spmd} | conditional | flops 1354498048 | bytes 35676240 | solution.py:193
  160.0 1.7 fusion.23
  161.7 1.2 convolution_add_fusion
  164.7 3.3 constant_dynamic-update-slice_fusion
  168.0 4.6 %copy.91 = bf16[2048,512]{1,0:T(8,128)(2,1)} copy(f32[2048,512]{0,1:T(8,128)} %get-tuple-element.990) | data formatting | bytes 6291456 | tf_op jit(solution)/shard_map/while | solution.py:75
  172.6 4.6 %copy.90 = bf16[2048,512]{1,0:T(8,128)(2,1)} copy(f32[2048,512]{0,1:T(8,128)} %get-tuple-element.989) | data formatting | bytes 6291456 | tf_op jit(solution)/shard_map/while | solution.py:75
  177.2 4.7 %pad_maximum_fusion = bf16[2048,1024]{1,0:T(8,128)(2,1)} fusion(bf16[2048,512]{1,0:T(8,128)(2,1)} %copy.91, bf16[2048,512]{1,0:T(8,128)(2,1)} %copy.90), kind=kLoop, calls=%fused_computation.90 | loop fusion | flops 8388608 | bytes 8388608 | tf_op jit(solution)/shard_map/concatenate | solution.py:21
  182.5 69.4 %reduce-scatter.2.cloned.1.call-done = bf16[128,1024]{1,0:T(8,128)(2,1)} async-done(((bf16[2048,1024]{1,0:T(8,128)(2,1)}), bf16[128,1024]{1,0:T(8,128)(2,1)}) %reduce-scatter.2.cloned.1.call-update) | async-done | bytes 262160 | tf_op jit(solution)/shard_map/reduce_scatter | solution.py:22
  251.9 1.7 slice_convert_fusion
  255.9 1.6 copy.92
  258.2 26.5 %all_to_all.23 = bf16[128,16,256]{0,1,2:T(8,128)(2,1)S(1)} all-to-all(bf16[128,16,256]{0,1,2:T(8,128)(2,1)S(1)} %copy.93), channel_id=1, replica_groups=mesh['dp'=16,'blk'=16] {'blk'}, dimensions={2} | all-to-all | bytes 2097152 | tf_op jit(solution)/shard_map/all_to_all | solution.py:242
  285.4 18.4 %all-gather.5.cloned.1.call-done = bf16[2048,1024]{1,0:T(8,128)(2,1)} async-done(((bf16[128,1024]{1,0:T(8,128)(2,1)}), bf16[2048,1024]{1,0:T(8,128)(2,1)}) %all-gather.5.cloned.1.call-update) | async-done | bytes 4194320 | tf_op jit(solution)/shard_map/all_gather | solution.py:246
  303.8 3.4 %fusion.47 = f32[1024,256]{0,1:S(1)} fusion(bf16[2048,1024]{1,0:T(8,128)(2,1)} %all-gather.5.cloned.1.call-done, bf16[32,8,16,128]{3,2,1,0:T(8,128)(2,1)S(1)} %bitcast.122), kind=kOutput, calls=%fused_computation.91 | convolution fusion | flops 1073741824 | bytes 6291456
  308.1 8.5 %all-to-all-start.1 = ((bf16[16,1,16,1024]{3,2,1,0:T(8,128)(2,1)}), bf16[16,1,16,1024]{3,2,1,0:T(8,128)(2,1)S(1)}, u32[]{:S(2)}, u32[]{:S(2)}) async-start(bf16[16,1,16,1024]{3,2,1,0:T(8,128)(2,1)} %convert_bitcast_fusion), calls=%async_computation.2 | async-start | bytes 1048576 | tf_op jit(solution)/shard_map/all_to_all | solution.py:33
  317.2 1.2 convert_element_type.92
  318.4 14.8 %all-to-all-done.1 = bf16[16,1,16,1024]{3,2,1,0:T(8,128)(2,1)S(1)} async-done(((bf16[16,1,16,1024]{3,2,1,0:T(8,128)(2,1)}), bf16[16,1,16,1024]{3,2,1,0:T(8,128)(2,1)S(1)}, u32[]{:S(2)}, u32[]{:S(2)}) %all-to-all-start.1) | async-done | bytes 524320 | tf_op jit(solution)/shard_map/all_to_all | solution.py:33
  (117 shorter events, 53.5 us)
Async XLA Ops:
  7.2 5.5 %copy-start.1 = (bf16[1,128,2048]{2,1,0:T(8,128)(2,1)S(1)}, bf16[1,128,2048]{2,1,0:T(8,128)(2,1)}, u32[]{:S(2)}) copy-start(bf16[1,128,2048]{2,1,0:T(8,128)(2,1)} %param.17) | copy-start | bytes 1572868
  7.2 56.1 %all-gather.3.cloned.1.call-start = ((), (), s32[]{:S(2)}) async-start(), calls=%async_computation.3 | async-start | bytes 4456448 | tf_op jit(solution)/shard_map/all_gather | solution.py:15
  8.3 6.3 %copy-start.2 = (s32[1,3]{1,0:T(1,128)S(1)}, s32[1,3]{1,0:T(1,128)}, u32[]{:S(2)}) copy-start(s32[1,3]{1,0:T(1,128)} %param.19) | copy-start | bytes 40
  10.1 241.8 %reduce-scatter.2.cloned.1.call-start = ((), (), s32[]{:S(2)}) async-start(), calls=%async_computation.4 | async-start | bytes 4456448 | tf_op jit(solution)/shard_map/reduce_scatter | solution.py:22
  109.7 5.0 %copy-start = (bf16[4,512,128]{1,2,0:T(8,128)(2,1)S(1)}, bf16[4,512,128]{1,2,0:T(8,128)(2,1)}, u32[]{:S(2)}) copy-start(bf16[4,512,128]{1,2,0:T(8,128)(2,1)} %reshape.344) | copy-start | bytes 1572868
  182.0 121.8 %all-gather.5.cloned.1.call-start = ((), (), s32[]{:S(2)}) async-start(), calls=%async_computation.5 | async-start | bytes 4456448 | tf_op jit(solution)/shard_map/all_gather | solution.py:246
  308.1 25.1 %all-to-all-start.1 = ((bf16[16,1,16,1024]{3,2,1,0:T(8,128)(2,1)}), bf16[16,1,16,1024]{3,2,1,0:T(8,128)(2,1)S(1)}, u32[]{:S(2)}, u32[]{:S(2)}) async-start(bf16[16,1,16,1024]{3,2,1,0:T(8,128)(2,1)} %convert_bitcast_fusion), calls=%async_computation.2 | async-start | bytes 1048576 | tf_op jit(solution)/shard_map/all_to_all | solution.py:33
Sparse Core Ops, SparseCore 0:
  10.2 53.0 all-gather.2
  182.1 69.7 reduce-scatter.1
  256.0 47.7 all-gather.4
where the time goes:
time: 342 us; the launch traced here: 340 us
  waiting for transfers between devices  149 us (44%)
  matrix products  47 us (14%)
  local copies, waits for them, and re-layouts  45 us (13%)
  other arithmetic  42.9 us (13%)
  blocking collectives  26.5 us (8%)
  between operations  15.3 us (4%)
  starting transfers between devices  8.67 us (3%)
  loops' own time  5.55 us (2%)
    reduce_scatter x1, waiting for transfers between devices, in_one_piece(): whole = lax.psum_scatter(both, axis, scatter_dimension=dim, tiled=True)  69.4 us
    all_gather x1, waiting for transfers between devices, side_by_side(): whole = lax.all_gather(both, axis, axis=dim, tiled=True)  46.8 us
    all_to_all x1, blocking collectives, body(): lax.all_to_all(grouped_input, 'blk', split_axis=2, concat_axis=0, tiled=T...  26.5 us
    all_gather x1, waiting for transfers between devices, body(): lax.all_gather(grad_cols, 'blk', axis=0, tiled=True)  18.4 us
    dot_general x4, matrix products, forward_compute(): jnp.einsum('gqk,kge->gqe', weights, value_heads, precision=lax.Precision....  17.7 us
    all_to_all x1, waiting for transfers between devices, sum_at_owner(): lax.all_to_all(pieces, axis, split_axis=0, concat_axis=0, tiled=True)  14.8 us
    dynamic_slice x12, local copies, waits for them, and re-layouts, one_turn(): lax.dynamic_slice_in_dim(member, block_start, block_rows, 0)  13.8 us
    dynamic_update_slice x4, other arithmetic, backward_compute(): lax.dynamic_update_slice_in_dim(key_acc, lax.dynamic_slice_in_dim(key_acc...  13 us
  transfers between devices with their start and end apart: 4, of which 4 were waited for; matrix products, arithmetic and copies ran while one was open for 3% of the time, Pallas kernels for 0%

commit v1 on v0

--- a/solution.py
+++ b/solution.py
@@ -243,7 +243,9 @@
     sequence_weight = jnp.einsum(
         "tif,tc->ifc",
         sequence_input,
-        lax.all_gather(grad_cols, "blk", axis=0, tiled=True),
+        jnp.concatenate(
+            lax.all_to_all(jnp.stack([grad_cols] * lax.axis_size("blk")), "blk", 0, 0), axis=0
+        ),
         preferred_element_type=jnp.float32,
     )
     weight_grad = sum_at_owner(sequence_weight.astype(jnp.bfloat16), "dp", 0).reshape(

time: 342 us -> 365 us (1.067)
  blocking collectives: 26.5 us -> 0 us
  waiting for transfers between devices: 149 us -> 175 us
  local copies, waits for them, and re-layouts: 45 us -> 55.8 us
  starting transfers between devices: 8.67 us -> 18.9 us
    all_to_all x0 -> x2, waiting for transfers between devices: none -> 48.3 us  [the longest x1 48.3 us: body(): lax.all_to_all(jnp.stack([grad_cols] * lax.axis_size('blk')), 'blk', 0, 0)]
    all_to_all x1 -> x0, blocking collectives: 26.5 us -> none  [body(): lax.all_to_all(grouped_input, 'blk', split_axis=2, concat_axis=0, tiled=T...]
    all_gather x1 -> x0, waiting for transfers between devices: 18.4 us -> none  [body(): lax.all_gather(grad_cols, 'blk', axis=0, tiled=True)]
    all_to_all x0 -> x2, starting transfers between devices: none -> 11 us  [the longest x1 7.24 us: body(): lax.all_to_all(jnp.stack([grad_cols] * lax.axis_size('blk')), 'blk', 0, 0)]
    dot_general x0 -> x1, matrix products: none -> 4.54 us  [body(): jnp.einsum('tif,tc->ifc', sequence_input, jnp.concatenate(lax.all_to_all(...]
    cond x4 -> x20, local copies, waits for them, and re-layouts: 0.01 us -> 3.92 us
    another operation x4 -> x5, local copies, waits for them, and re-layouts: 5.09 us -> 8.6 us
  transfers between devices with their start and end apart: 4 -> 5, of which waited for: 4 -> 4; matrix products, arithmetic and copies ran while one was open for 3% -> 4% of each run, Pallas kernels for 0% -> 0%
where the time goes in v1:
time: 365 us; the launch traced here: 360 us
  waiting for transfers between devices  175 us (48%)
  local copies, waits for them, and re-layouts  55.8 us (15%)
  matrix products  48.1 us (13%)
  other arithmetic  41.4 us (11%)
  starting transfers between devices  18.9 us (5%)
  between operations  15.6 us (4%)
  loops' own time  5.28 us (1%)
    reduce_scatter x1, waiting for transfers between devices, in_one_piece(): whole = lax.psum_scatter(both, axis, scatter_dimension=dim, tiled=True)  68.6 us
    all_to_all x1, waiting for transfers between devices, body(): lax.all_to_all(jnp.stack([grad_cols] * lax.axis_size('blk')), 'blk', 0, 0)  48.3 us
    all_gather x1, waiting for transfers between devices, side_by_side(): whole = lax.all_gather(both, axis, axis=dim, tiled=True)  46.8 us
    dot_general x4, matrix products, forward_compute(): jnp.einsum('gqk,kge->gqe', weights, value_heads, precision=lax.Precision....  17.7 us
    dynamic_slice x12, local copies, waits for them, and re-layouts, one_turn(): lax.dynamic_slice_in_dim(member, block_start, block_rows, 0)  13.2 us
    dynamic_update_slice x4, other arithmetic, backward_compute(): lax.dynamic_update_slice_in_dim(key_acc, lax.dynamic_slice_in_dim(key_acc...  13 us
    while x3, local copies, waits for them, and re-layouts, over_blocks(): return lax.fori_loop(0, total_rows // block_rows, one_turn, running)  12.5 us
    all_to_all x1, waiting for transfers between devices, sum_at_owner(): lax.all_to_all(pieces, axis, split_axis=0, concat_axis=0, tiled=True)  11.8 us
  transfers between devices with their start and end apart: 5, of which 4 were waited for; matrix products, arithmetic and copies ran while one was open for 4% of the time, Pallas kernels for 0%

profile of v1, /device:TPU:1, one launch (start us, length us, event | category | flops | bytes accessed | tf_op | source)
XLA Modules:
  0.0 360.4 jit_solution(15649504833109046702)
XLA Ops:
  10.2 1.4 reshape_squeeze.9
  16.5 46.8 %all-gather.2.cloned.1.call-done = bf16[2048,1024]{0,1:T(8,128)(2,1)} async-done(((bf16[128,1024]{0,1:T(8,128)(2,1)}), bf16[2048,1024]{0,1:T(8,128)(2,1)}) %all-gather.2.cloned.1.call-update) | async-done | bytes 4194320 | tf_op jit(solution)/shard_map/all_gather | solution.py:15
  63.3 4.1 %fusion.63 = (bf16[2048,512]{0,1:T(8,128)(2,1)S(1)}, bf16[2048,512]{0,1:T(8,128)(2,1)}) fusion(bf16[2048,1024]{0,1:T(8,128)(2,1)} %all-gather.2.cloned.1.call-done), kind=kLoop, calls=%fused_computation.130 | loop fusion | bytes 8388608 | tf_op jit(solution)/shard_map/split | solution.py:16
  68.4 43.1 %while.44 = (s32[]{:T(128)}, f32[4,512]{1,0:T(4,128)S(1)}, f32[4,512]{1,0:T(4,128)S(1)}, f32[4,512,128]{2,1,0:T(8,128)}, s32[]{:T(128)}, /*index=5*/s32[]{:T(128...) while((s32[]{:T(128)}, f32[4,512]{1,0:T(4,128)S(1)}, ...), condition=%wide.region_6.7_spmd.clone.clone, body=%wide.region_0.6_spmd.clone.clone.sunk | while | flops 1891420160 | bytes 27929972 | solution.py:75
  70.6 8.6 %conditional.8 = ((f32[4,512]{1,0:T(4,128)S(1)}, f32[4,512]{1,0:T(4,128)S(1)}, f32[4,512,128]{2,1,0:T(8,128)})) conditional(s32[]{:T(128)} %convert_element_type.120, (f32[4,512]{1,0:T(4,128)S(1)}, f32[4,512]{1,0:T(4,128)S(1)}, f32[4,512,128]{2,1,0:T(8,128)}) %tuple.160, (pred[512,512]{0,1:T(8,128)(4,1)S(1)}, s32[]{:T(128)}, ...), branch_computations={%region_2.2_spmd, %region_3.5_spmd} | conditional | flops 1890062336 | bytes 27656318 | solution.py:138
  73.7 4.4 %fusion.18 = f32[4,512,128]{2,1,0:T(8,128)S(1)} fusion(bf16[512,4,128]{0,2,1:T(8,128)(2,1)S(1)} %bitcast.119, f32[4,512,512]{2,1,0:T(8,128)S(1)} %get-tuple-element.1214, f32[4,512]{1,0:T(4,128)S(1)} %max.5, pred[512,512]{0,1:T(8,128)(4,1)S(1)} %get-tuple-element.924, f32[4,512,128]{2,1,0:T(8,128)S(1)} %copy-done.1, f32[4,512]{1,0:T(4,128)S(1)} %get-tuple-element.1206), kind=kOutput, calls=%fused_computation.15 | convolution fusion | flops 1614282752 | bytes 7094272 | tf_op jit(solution)/shard_map/while/body/eval_jaxpr/cond/branch_1_fun/gqk,kge->gqe/dot_general | solution.py:133
  81.4 8.6 %conditional.8 = ((f32[4,512]{1,0:T(4,128)S(1)}, f32[4,512]{1,0:T(4,128)S(1)}, f32[4,512,128]{2,1,0:T(8,128)})) conditional(s32[]{:T(128)} %convert_element_type.120, (f32[4,512]{1,0:T(4,128)S(1)}, f32[4,512]{1,0:T(4,128)S(1)}, f32[4,512,128]{2,1,0:T(8,128)}) %tuple.160, (pred[512,512]{0,1:T(8,128)(4,1)S(1)}, s32[]{:T(128)}, ...), branch_computations={%region_2.2_spmd, %region_3.5_spmd} | conditional | flops 1890062336 | bytes 27656318 | solution.py:138
  84.5 4.4 %fusion.18 = f32[4,512,128]{2,1,0:T(8,128)S(1)} fusion(bf16[512,4,128]{0,2,1:T(8,128)(2,1)S(1)} %bitcast.119, f32[4,512,512]{2,1,0:T(8,128)S(1)} %get-tuple-element.1214, f32[4,512]{1,0:T(4,128)S(1)} %max.5, pred[512,512]{0,1:T(8,128)(4,1)S(1)} %get-tuple-element.924, f32[4,512,128]{2,1,0:T(8,128)S(1)} %copy-done.1, f32[4,512]{1,0:T(4,128)S(1)} %get-tuple-element.1206), kind=kOutput, calls=%fused_computation.15 | convolution fusion | flops 1614282752 | bytes 7094272 | tf_op jit(solution)/shard_map/while/body/eval_jaxpr/cond/branch_1_fun/gqk,kge->gqe/dot_general | solution.py:133
  92.2 8.6 %conditional.8 = ((f32[4,512]{1,0:T(4,128)S(1)}, f32[4,512]{1,0:T(4,128)S(1)}, f32[4,512,128]{2,1,0:T(8,128)})) conditional(s32[]{:T(128)} %convert_element_type.120, (f32[4,512]{1,0:T(4,128)S(1)}, f32[4,512]{1,0:T(4,128)S(1)}, f32[4,512,128]{2,1,0:T(8,128)}) %tuple.160, (pred[512,512]{0,1:T(8,128)(4,1)S(1)}, s32[]{:T(128)}, ...), branch_computations={%region_2.2_spmd, %region_3.5_spmd} | conditional | flops 1890062336 | bytes 27656318 | solution.py:138
  95.3 4.4 %fusion.18 = f32[4,512,128]{2,1,0:T(8,128)S(1)} fusion(bf16[512,4,128]{0,2,1:T(8,128)(2,1)S(1)} %bitcast.119, f32[4,512,512]{2,1,0:T(8,128)S(1)} %get-tuple-element.1214, f32[4,512]{1,0:T(4,128)S(1)} %max.5, pred[512,512]{0,1:T(8,128)(4,1)S(1)} %get-tuple-element.924, f32[4,512,128]{2,1,0:T(8,128)S(1)} %copy-done.1, f32[4,512]{1,0:T(4,128)S(1)} %get-tuple-element.1206), kind=kOutput, calls=%fused_computation.15 | convolution fusion | flops 1614282752 | bytes 7094272 | tf_op jit(solution)/shard_map/while/body/eval_jaxpr/cond/branch_1_fun/gqk,kge->gqe/dot_general | solution.py:133
  102.9 8.6 %conditional.8 = ((f32[4,512]{1,0:T(4,128)S(1)}, f32[4,512]{1,0:T(4,128)S(1)}, f32[4,512,128]{2,1,0:T(8,128)})) conditional(s32[]{:T(128)} %convert_element_type.120, (f32[4,512]{1,0:T(4,128)S(1)}, f32[4,512]{1,0:T(4,128)S(1)}, f32[4,512,128]{2,1,0:T(8,128)}) %tuple.160, (pred[512,512]{0,1:T(8,128)(4,1)S(1)}, s32[]{:T(128)}, ...), branch_computations={%region_2.2_spmd, %region_3.5_spmd} | conditional | flops 1890062336 | bytes 27656318 | solution.py:138
  106.1 4.4 %fusion.18 = f32[4,512,128]{2,1,0:T(8,128)S(1)} fusion(bf16[512,4,128]{0,2,1:T(8,128)(2,1)S(1)} %bitcast.119, f32[4,512,512]{2,1,0:T(8,128)S(1)} %get-tuple-element.1214, f32[4,512]{1,0:T(4,128)S(1)} %max.5, pred[512,512]{0,1:T(8,128)(4,1)S(1)} %get-tuple-element.924, f32[4,512,128]{2,1,0:T(8,128)S(1)} %copy-done.1, f32[4,512]{1,0:T(4,128)S(1)} %get-tuple-element.1206), kind=kOutput, calls=%fused_computation.15 | convolution fusion | flops 1614282752 | bytes 7094272 | tf_op jit(solution)/shard_map/while/body/eval_jaxpr/cond/branch_1_fun/gqk,kge->gqe/dot_general | solution.py:133
  111.5 3.3 copy.87
  114.8 1.6 multiply_reduce_fusion
  116.5 2.5 broadcast.1269
  119.0 2.5 broadcast.1269.clone
  121.5 52.9 %while.45 = (s32[]{:T(128)}, f32[4,512,128]{2,1,0:T(8,128)S(1)}, f32[2048,512]{0,1:T(8,128)}, f32[2048,512]{0,1:T(8,128)}, s32[]{:T(128)}, /*index=5*/s32[]{:T(1...) while((s32[]{:T(128)}, f32[4,512,128]{2,1,0:T(8,128)S(1)}, ...), condition=%wide.region_12.13_spmd.clone.clone, body=%wide.region_8.12_spmd.clone.clone.sunk | while | flops 1355855872 | bytes 35949944 | solution.py:75
  123.7 11.0 %conditional.9 = ((f32[4,512,128]{2,1,0:T(8,128)S(1)}, f32[2048,512]{0,1:T(8,128)}, f32[2048,512]{0,1:T(8,128)})) conditional(s32[]{:T(128)} %convert_element_type.121, (f32[4,512,128]{2,1,0:T(8,128)S(1)}, f32[2048,512]{0,1:T(8,128)}, f32[2048,512]{0,1:T(8,128)}) %tuple.165, (pred[512,512]{0,1:T(8,128)(4,1)S(1)}, s32[]{:T(128)}, ...), branch_computations={%region_10.10_spmd, %region_11.11_spmd} | conditional | flops 1354498048 | bytes 35676240 | solution.py:193
  126.7 1.7 fusion.23
  128.3 1.2 convolution_add_fusion
  131.4 3.3 constant_dynamic-update-slice_fusion
  137.0 11.0 %conditional.9 = ((f32[4,512,128]{2,1,0:T(8,128)S(1)}, f32[2048,512]{0,1:T(8,128)}, f32[2048,512]{0,1:T(8,128)})) conditional(s32[]{:T(128)} %convert_element_type.121, (f32[4,512,128]{2,1,0:T(8,128)S(1)}, f32[2048,512]{0,1:T(8,128)}, f32[2048,512]{0,1:T(8,128)}) %tuple.165, (pred[512,512]{0,1:T(8,128)(4,1)S(1)}, s32[]{:T(128)}, ...), branch_computations={%region_10.10_spmd, %region_11.11_spmd} | conditional | flops 1354498048 | bytes 35676240 | solution.py:193
  139.9 1.7 fusion.23
  141.6 1.2 convolution_add_fusion
  144.6 3.3 constant_dynamic-update-slice_fusion
  150.2 10.9 %conditional.9 = ((f32[4,512,128]{2,1,0:T(8,128)S(1)}, f32[2048,512]{0,1:T(8,128)}, f32[2048,512]{0,1:T(8,128)})) conditional(s32[]{:T(128)} %convert_element_type.121, (f32[4,512,128]{2,1,0:T(8,128)S(1)}, f32[2048,512]{0,1:T(8,128)}, f32[2048,512]{0,1:T(8,128)}) %tuple.165, (pred[512,512]{0,1:T(8,128)(4,1)S(1)}, s32[]{:T(128)}, ...), branch_computations={%region_10.10_spmd, %region_11.11_spmd} | conditional | flops 1354498048 | bytes 35676240 | solution.py:193
  153.1 1.7 fusion.23
  154.8 1.2 convolution_add_fusion
  157.9 3.2 constant_dynamic-update-slice_fusion
  163.4 11.0 %conditional.9 = ((f32[4,512,128]{2,1,0:T(8,128)S(1)}, f32[2048,512]{0,1:T(8,128)}, f32[2048,512]{0,1:T(8,128)})) conditional(s32[]{:T(128)} %convert_element_type.121, (f32[4,512,128]{2,1,0:T(8,128)S(1)}, f32[2048,512]{0,1:T(8,128)}, f32[2048,512]{0,1:T(8,128)}) %tuple.165, (pred[512,512]{0,1:T(8,128)(4,1)S(1)}, s32[]{:T(128)}, ...), branch_computations={%region_10.10_spmd, %region_11.11_spmd} | conditional | flops 1354498048 | bytes 35676240 | solution.py:193
  166.3 1.7 fusion.23
  168.0 1.2 convolution_add_fusion
  171.1 3.3 constant_dynamic-update-slice_fusion
  174.3 4.6 %copy.90 = bf16[2048,512]{1,0:T(8,128)(2,1)} copy(f32[2048,512]{0,1:T(8,128)} %get-tuple-element.990) | data formatting | bytes 6291456 | tf_op jit(solution)/shard_map/while | solution.py:75
  178.9 4.6 %copy.89 = bf16[2048,512]{1,0:T(8,128)(2,1)} copy(f32[2048,512]{0,1:T(8,128)} %get-tuple-element.989) | data formatting | bytes 6291456 | tf_op jit(solution)/shard_map/while | solution.py:75
  183.6 4.7 %pad_maximum_fusion = bf16[2048,1024]{1,0:T(8,128)(2,1)} fusion(bf16[2048,512]{1,0:T(8,128)(2,1)} %copy.90, bf16[2048,512]{1,0:T(8,128)(2,1)} %copy.89), kind=kLoop, calls=%fused_computation.90 | loop fusion | flops 8388608 | bytes 8388608 | tf_op jit(solution)/shard_map/concatenate | solution.py:21
  188.3 1.6 copy.91
  189.9 1.6 copy.92
  191.6 3.7 %all-to-all-start.1 = ((bf16[128,16,256]{0,1,2:T(8,128)(2,1)}), bf16[128,16,256]{0,1,2:T(8,128)(2,1)S(1)}, u32[]{:S(2)}, u32[]{:S(2)}) async-start(bf16[128,16,256]{0,1,2:T(8,128)(2,1)} %copy.92), calls=%async_computation.2 | async-start | bytes 2097152 | tf_op jit(solution)/shard_map/all_to_all | solution.py:242
  195.8 68.6 %reduce-scatter.2.cloned.1.call-done = bf16[128,1024]{1,0:T(8,128)(2,1)} async-done(((bf16[2048,1024]{1,0:T(8,128)(2,1)}), bf16[128,1024]{1,0:T(8,128)(2,1)}) %reduce-scatter.2.cloned.1.call-update) | async-done | bytes 262160 | tf_op jit(solution)/shard_map/reduce_scatter | solution.py:22
  264.3 1.7 slice_convert_fusion
  267.6 2.5 stack.2
  270.1 7.2 %all-to-all-start = ((bf16[16,128,1024]{2,1,0:T(8,128)(2,1)}), bf16[16,128,1024]{2,1,0:T(8,128)(2,1)}, u32[]{:S(2)}, u32[]{:S(2)}) async-start(bf16[16,128,1024]{2,1,0:T(8,128)(2,1)} %stack.2), calls=%async_computation.1 | async-start | bytes 8388608 | tf_op jit(solution)/shard_map/all_to_all | solution.py:247
  277.4 1.3 copy.93
  278.7 48.3 %all-to-all-done = bf16[16,128,1024]{2,1,0:T(8,128)(2,1)} async-done(((bf16[16,128,1024]{2,1,0:T(8,128)(2,1)}), bf16[16,128,1024]{2,1,0:T(8,128)(2,1)}, u32[]{:S(2)}, u32[]{:S(2)}) %all-to-all-start) | async-done | bytes 4194336 | tf_op jit(solution)/shard_map/all_to_all | solution.py:247
  327.0 4.5 %fusion.55 = bf16[16,1,16,1024]{3,2,1,0:T(8,128)(2,1)} fusion(bf16[16,128,16,16]{1,3,0,2:T(8,128)(2,1)} %bitcast.128, bf16[16,128,1024]{2,1,0:T(8,128)(2,1)} %all-to-all-done), kind=kOutput, calls=%fused_computation.95 | convolution fusion | flops 1074003968 | bytes 5767168 | tf_op jit(solution)/shard_map/tif,tc->ifc/dot_general | solution.py:243
  331.5 7.8 %all-to-all-start.2 = ((bf16[16,1,16,1024]{3,2,1,0:T(8,128)(2,1)}), bf16[16,1,16,1024]{3,2,1,0:T(8,128)(2,1)S(1)}, u32[]{:S(2)}, u32[]{:S(2)}) async-start(bf16[16,1,16,1024]{3,2,1,0:T(8,128)(2,1)} %fusion.55), calls=%async_computation.3 | async-start | bytes 1048576 | tf_op jit(solution)/shard_map/all_to_all | solution.py:33
  341.1 11.8 %all-to-all-done.2 = bf16[16,1,16,1024]{3,2,1,0:T(8,128)(2,1)S(1)} async-done(((bf16[16,1,16,1024]{3,2,1,0:T(8,128)(2,1)}), bf16[16,1,16,1024]{3,2,1,0:T(8,128)(2,1)S(1)}, u32[]{:S(2)}, u32[]{:S(2)}) %all-to-all-start.2) | async-done | bytes 524320 | tf_op jit(solution)/shard_map/all_to_all | solution.py:33
  (135 shorter events, 60.6 us)
Async XLA Ops:
  7.2 5.5 %copy-start.4 = (bf16[1,128,2048]{2,1,0:T(8,128)(2,1)S(1)}, bf16[1,128,2048]{2,1,0:T(8,128)(2,1)}, u32[]{:S(2)}) copy-start(bf16[1,128,2048]{2,1,0:T(8,128)(2,1)} %param.17) | copy-start | bytes 1572868
  7.2 56.1 %all-gather.2.cloned.1.call-start = ((), (), s32[]{:S(2)}) async-start(), calls=%async_computation.4 | async-start | bytes 4456448 | tf_op jit(solution)/shard_map/all_gather | solution.py:15
  8.3 6.3 %copy-start.5 = (s32[1,3]{1,0:T(1,128)S(1)}, s32[1,3]{1,0:T(1,128)}, u32[]{:S(2)}) copy-start(s32[1,3]{1,0:T(1,128)} %param.19) | copy-start | bytes 40
  10.1 254.2 %reduce-scatter.2.cloned.1.call-start = ((), (), s32[]{:S(2)}) async-start(), calls=%async_computation.5 | async-start | bytes 4456448 | tf_op jit(solution)/shard_map/reduce_scatter | solution.py:22
  71.8 2.0 copy-start.1
  78.2 1.0 copy-start.2
  82.5 2.0 copy-start.1
  89.0 1.0 copy-start.2
  93.3 2.0 copy-start.1
  99.7 1.0 copy-start.2
  104.1 2.0 copy-start.1
  110.5 1.0 copy-start.2
  111.5 3.3 copy-start
  116.5 5.0 %copy-start.3 = (bf16[4,512,128]{1,2,0:T(8,128)(2,1)S(1)}, bf16[4,512,128]{1,2,0:T(8,128)(2,1)}, u32[]{:S(2)}) copy-start(bf16[4,512,128]{1,2,0:T(8,128)(2,1)} %reshape.347) | copy-start | bytes 1572868
  191.6 76.0 %all-to-all-start.1 = ((bf16[128,16,256]{0,1,2:T(8,128)(2,1)}), bf16[128,16,256]{0,1,2:T(8,128)(2,1)S(1)}, u32[]{:S(2)}, u32[]{:S(2)}) async-start(bf16[128,16,256]{0,1,2:T(8,128)(2,1)} %copy.92), calls=%async_computation.2 | async-start | bytes 2097152 | tf_op jit(solution)/shard_map/all_to_all | solution.py:242
  270.1 56.9 %all-to-all-start = ((bf16[16,128,1024]{2,1,0:T(8,128)(2,1)}), bf16[16,128,1024]{2,1,0:T(8,128)(2,1)}, u32[]{:S(2)}, u32[]{:S(2)}) async-start(bf16[16,128,1024]{2,1,0:T(8,128)(2,1)} %stack.2), calls=%async_computation.1 | async-start | bytes 8388608 | tf_op jit(solution)/shard_map/all_to_all | solution.py:247
  331.5 21.4 %all-to-all-start.2 = ((bf16[16,1,16,1024]{3,2,1,0:T(8,128)(2,1)}), bf16[16,1,16,1024]{3,2,1,0:T(8,128)(2,1)S(1)}, u32[]{:S(2)}, u32[]{:S(2)}) async-start(bf16[16,1,16,1024]{3,2,1,0:T(8,128)(2,1)} %fusion.55), calls=%async_computation.3 | async-start | bytes 1048576 | tf_op jit(solution)/shard_map/all_to_all | solution.py:33
Sparse Core Ops, SparseCore 0:
  10.2 53.0 all-gather.1
  188.4 75.8 reduce-scatter.1
